TPU v7x, 32 devices: a whole 2x2x4 slice. The times are simulated.
32 devices in a mesh: groups: 2 (over x), seq: 4 (over y, core), head: 4 (over z).
Axes of the slice: x: 2, y: 2, z: 4, core: 2. Of those that a mesh axis runs over, the one named last changes fastest.
Arguments:
- queries: bfloat16 [1024, 8192], P(('groups', 'seq'), 'head'), parts along dimension 0
- new_keys: bfloat16 [1024, 1024], P(('groups', 'seq'), 'head'), parts along dimension 0, may hold values from -6 to 6
- new_values: bfloat16 [1024, 1024], P(('groups', 'seq'), 'head'), parts along dimension 0, may hold values from -6 to 6
- cache_keys: bfloat16 [8192, 1024], P(('groups', 'seq'), 'head'), parts along dimension 0
- cache_values: bfloat16 [8192, 1024], P(('groups', 'seq'), 'head'), parts along dimension 0, may hold values from -6 to 6
- valid_len: int32 [8], P('groups'), parts along dimension 0, may hold values from 1 to 1024, as said below
- block_of: int32 [8], P('groups'), parts along dimension 0, may hold values from 0 to 3, each once
Outputs:
- attended: bfloat16 [1024, 8192], P(('groups', 'seq'), 'head'), parts along dimension 0
There are 2 independent parts, one for each index of `groups`. A program takes and returns all parts, laid end to end along the dimension named above; each array names one. Nothing has to cross between parts.
Inputs may be any that keep to these rules, and one draw needn't show every extreme that they name: `valid_len`: some shard is full (1024 filled slots) in every draw; slot 0 of every shard is filled. `block_of`: A permutation of the 4 span blocks.
All inputs are finite; a program needn't handle non-finite values.
Results may differ from a plain program's by a relative error of at most 0.0027.
Values may be sent and summed in bfloat16 or wider, within the bound.
A program may use at most 192 MiB of HBM per device.

v0:
```python
import functools
import math

import jax
import jax.numpy as jnp
from jax import lax
from jax.experimental import pallas as pl
from jax.experimental.pallas import tpu as pltpu
from jax.sharding import PartitionSpec as P

DH = 128
GROUP = 8
NEGATIVE = -1e30
TO_LOG2 = DH ** (-0.5) * math.log2(math.e)
CODE_MAX = 32767.0
UNROLL = 2


def kernel(
    n, pair, chunk,
    q_hbm, nk_hbm, nv_hbm, ck_hbm, cv_hbm, valid_ref, block_ref,
    out_ref,
    kbuf, vbuf, qbuf, numer, stats, code_out, code_in, stat_out, stat_in,
    cache_bias, span_bias, pad,
    loc_sem, kv_send, kv_recv, q_send, q_recv, r_send, r_recv, s_send, s_recv,
):
    chips = n // pair
    rows, cols = q_hbm.shape
    length = ck_hbm.shape[0]
    per = length + rows
    heads = cols // DH
    chunks = heads // chunk
    width = chunk * DH
    me = lax.axis_index("seq")
    chip, core = me // pair, me % pair
    partner = chip * pair + (pair - 1 - core)

    def ahead(d):
        return ((chip + d) % chips) * pair + core

    def behind(d):
        return ((chip + chips - d) % chips) * pair + core

    sources = (ck_hbm, nk_hbm, cv_hbm, nv_hbm)
    spans = ((0, length), (length, rows))

    def place(i, slot):
        buf = kbuf if i < 2 else vbuf
        start, size = spans[i % 2]
        return buf.at[pl.ds(slot * per + start, size), :]

    local = [
        pltpu.make_async_copy(sources[i], place(i, 0), loc_sem.at[i]) for i in range(4)
    ] + [pltpu.make_async_copy(q_hbm, qbuf.at[0], loc_sem.at[4])]
    for copy in local:
        copy.start()

    barrier = pltpu.get_barrier_semaphore()
    others = [ahead(d) for d in range(1, chips)] + ([partner] if pair > 1 else [])
    for other in others:
        pl.semaphore_signal(barrier, inc=1, device_id={"seq": other})
    pl.semaphore_wait(barrier, len(others))

    def columns(c):
        return pl.ds(c * width, width)

    def send_query(d, c):
        return pltpu.make_async_remote_copy(
            src_ref=q_hbm.at[:, columns(c)],
            dst_ref=qbuf.at[d, :, columns(c)],
            send_sem=q_send.at[d, c], recv_sem=q_recv.at[d, c],
            device_id={"seq": ahead(d)},
        )

    def send_codes(d, c):
        return pltpu.make_async_remote_copy(
            src_ref=code_out.at[d, :, columns(c)],
            dst_ref=code_in.at[d, :, columns(c)],
            send_sem=r_send.at[d, c], recv_sem=r_recv.at[d, c],
            device_id={"seq": behind(d)},
        )

    def send_stats(d, c):
        return pltpu.make_async_remote_copy(
            src_ref=stat_out.at[d, c], dst_ref=stat_in.at[d, c],
            send_sem=s_send.at[d, c], recv_sem=s_recv.at[d, c],
            device_id={"seq": behind(d)},
        )

    query_copies = {(d, c): send_query(d, c) for c in range(chunks) for d in range(1, chips)}
    kv_copies = []
    if pair > 1:
        kv_copies = [
            pltpu.make_async_remote_copy(
                src_ref=sources[i], dst_ref=place(i, 1),
                send_sem=kv_send.at[i], recv_sem=kv_recv.at[i],
                device_id={"seq": partner},
            )
            for i in range(4)
        ]
    for (d, c), copy in query_copies.items():
        if c == 0:
            copy.start()
    for copy in kv_copies:
        copy.start()
    for (d, c), copy in query_copies.items():
        if c > 0:
            copy.start()

    key_owner = [me, partner][:pair]
    slot_at = lax.broadcasted_iota(jnp.int32, (8, length), 1)
    for slot in range(pair):
        live = slot_at < valid_ref[key_owner[slot]]
        cache_bias[slot] = jnp.where(live, 0.0, NEGATIVE)
    row_at = lax.broadcasted_iota(jnp.int32, (rows, rows), 0)
    col_at = lax.broadcasted_iota(jnp.int32, (rows, rows), 1)
    for d in range(chips):
        row_pos = block_ref[behind(d)] * rows + row_at
        for slot in range(pair):
            seen = block_ref[key_owner[slot]] * rows + col_at <= row_pos
            span_bias[d, slot] = jnp.where(seen, 0.0, NEGATIVE)

    lane = lax.broadcasted_iota(jnp.int32, (rows, DH), 1)
    pad[...] = jnp.zeros_like(pad)

    def head_terms(d, c, h):
        at = pl.ds(pl.multiple_of((c * chunk + h) * DH, DH), DH)
        head = (c * chunk) // GROUP
        kv_at = pl.ds(head * DH, DH)
        scores = lax.dot_general(
            qbuf[d, :, at], kbuf[:, kv_at], (((1,), (1,)), ((), ())),
            preferred_element_type=jnp.float32,
        )
        pieces = []
        for slot in range(pair):
            base = slot * per
            pieces.append(
                scores[:, base : base + length] * TO_LOG2 + cache_bias[slot, 0:1, :]
            )
            pieces.append(
                scores[:, base + length : base + per] * TO_LOG2 + span_bias[d, slot]
            )
        logits = jnp.concatenate(pieces, axis=1)
        top = jnp.max(logits, axis=1, keepdims=True)
        weights = jnp.exp2(logits - top)
        total = jnp.sum(weights, axis=1, keepdims=True)
        value = jnp.dot(
            weights.astype(jnp.bfloat16), vbuf[:, kv_at], preferred_element_type=jnp.float32
        )
        return at, top, total, value

    def own_chunk(c):
        def body(step, carry):
            for u in range(UNROLL):
                h = step * UNROLL + u
                at, top, total, value = head_terms(0, c, h)
                numer[:, at] = value
                stats[c, 0] = jnp.where(lane == h, top, stats[c, 0])
                stats[c, 1] = jnp.where(lane == h, total, stats[c, 1])
            return carry

        stats[c] = jnp.ones_like(stats[c])
        lax.fori_loop(0, chunk // UNROLL, body, 0)

    def other_chunk(d, c):
        def body(step, carry):
            for u in range(UNROLL):
                h = step * UNROLL + u
                at, top, total, value = head_terms(d, c, h)
                size = jnp.maximum(jnp.max(jnp.abs(value), axis=1, keepdims=True), 1e-30)
                code_out[d, :, at] = (
                    jnp.round(value * (CODE_MAX / size)).astype(jnp.int32).astype(jnp.int16)
                )
                pad[0] = jnp.where(lane == h, top, pad[0])
                pad[1] = jnp.where(lane == h, total, pad[1])
                pad[2] = jnp.where(lane == h, size * (1.0 / CODE_MAX), pad[2])
            return carry

        lax.fori_loop(0, chunk // UNROLL, body, 0)
        for k in range(3):
            stat_out[d, c, k] = jnp.transpose(pad[k])[0:8]
        send_codes(d, c).start()
        send_stats(d, c).start()

    for i in (0, 1, 4, 2, 3):
        local[i].wait()
    for copy in kv_copies:
        copy.wait()
    early = chunks // 2
    for c in range(early):
        own_chunk(c)
    for c in range(chunks):
        for d in range(1, chips):
            query_copies[d, c].wait_recv()
            other_chunk(d, c)
    for c in range(early, chunks):
        own_chunk(c)

    for c in range(chunks):
        mine_top, mine_total = stats[c, 0], stats[c, 1]
        got = []
        for d in range(1, chips):
            send_codes(d, c).wait_recv()
            send_stats(d, c).wait_recv()
            three = []
            for k in range(3):
                pad[k, 0:8] = stat_in[d, c, k]
                three.append(jnp.transpose(pad[k]))
            got.append(three)
        top = mine_top
        for three in got:
            top = jnp.maximum(top, three[0])
        own_factor = jnp.exp2(mine_top - top)
        total = own_factor * mine_total
        factors = [jnp.exp2(three[0] - top) for three in got]
        for factor, three in zip(factors, got):
            total = total + factor * three[1]
        inverse = 1.0 / total
        own_factor = own_factor * inverse
        factors = [factor * three[2] * inverse for factor, three in zip(factors, got)]
        for h in range(chunk):
            at = pl.ds((c * chunk + h) * DH, DH)
            result = numer[:, at] * own_factor[:, h : h + 1]
            for d in range(1, chips):
                codes = code_in[d, :, at].astype(jnp.int32).astype(jnp.float32)
                result = result + codes * factors[d - 1][:, h : h + 1]
            out_ref[:, at] = result.astype(jnp.bfloat16)

    for c in range(chunks):
        for d in range(1, chips):
            query_copies[d, c].wait_send()
            send_codes(d, c).wait_send()
            send_stats(d, c).wait_send()


def on_device(queries, new_keys, new_values, cache_keys, cache_values, valid_len, block_of):
    n = lax.axis_size("seq")
    pair = 2 if n % 2 == 0 else 1
    chips = n // pair
    rows, cols = queries.shape
    kv_cols = new_keys.shape[1]
    length = cache_keys.shape[0]
    heads = cols // DH
    chunk = 4
    chunks = heads // chunk
    everywhere = pl.BlockSpec(memory_space=pl.ANY)
    scalars = pl.BlockSpec(memory_space=pltpu.SMEM)
    dma = pltpu.SemaphoreType.DMA
    keys = pair * (length + rows)
    return pl.pallas_call(
        functools.partial(kernel, n, pair, chunk),
        out_shape=jax.ShapeDtypeStruct((rows, cols), jnp.bfloat16),
        in_specs=[everywhere] * 5 + [scalars] * 2,
        out_specs=pl.BlockSpec(memory_space=pltpu.VMEM),
        scratch_shapes=[
            pltpu.VMEM((keys, kv_cols), jnp.bfloat16),
            pltpu.VMEM((keys, kv_cols), jnp.bfloat16),
            pltpu.VMEM((chips, rows, cols), jnp.bfloat16),
            pltpu.VMEM((rows, cols), jnp.float32),
            pltpu.VMEM((chunks, 2, rows, DH), jnp.float32),
            pltpu.VMEM((chips, rows, cols), jnp.int16),
            pltpu.VMEM((chips, rows, cols), jnp.int16),
            pltpu.VMEM((chips, chunks, 3, 8, rows), jnp.float32),
            pltpu.VMEM((chips, chunks, 3, 8, rows), jnp.float32),
            pltpu.VMEM((pair, 8, length), jnp.float32),
            pltpu.VMEM((chips, pair, rows, rows), jnp.float32),
            pltpu.VMEM((3, rows, DH), jnp.float32),
            dma((5,)), dma((4,)), dma((4,)),
            dma((chips, chunks)), dma((chips, chunks)),
            dma((chips, chunks)), dma((chips, chunks)),
            dma((chips, chunks)), dma((chips, chunks)),
        ],
        compiler_params=pltpu.CompilerParams(collective_id=0, has_side_effects=True),
    )(queries, new_keys, new_values, cache_keys, cache_values, valid_len, block_of)


def solution(mesh):
    placed = (
        P(("groups", "seq"), "head"),
        P(("groups", "seq"), "head"),
        P(("groups", "seq"), "head"),
        P(("groups", "seq"), "head"),
        P(("groups", "seq"), "head"),
        P("groups"),
        P("groups"),
    )
    return jax.shard_map(
        on_device,
        mesh=mesh,
        in_specs=placed,
        out_specs=P(("groups", "seq"), "head"),
        check_vma=False,
    )
```

profile of v0, /device:TPU:1, one launch (start us, length us, event | category | flops | bytes accessed | tf_op | source)
XLA Modules:
  0.0 33.3 jit_solution(4814717172427212179)
XLA Ops:
  0.0 31.4 %shard_map.73 = bf16[128,2048]{1,0:T(8,128)(2,1)} custom-call(bf16[128,2048]{1,0:T(8,128)(2,1)} %q_hbm.1, bf16[128,256]{1,0:T(8,128)(2,1)} %nk_hbm.1, bf16[128,256]{1,0:T(8,128)(2,1)} %nv_hbm.1, bf16[1024,256]{1,0:T(8,128)(2,1)} %ck_hbm.1, bf16[1024,256]{1,0:T(8,128)(2,1)} %cv_hbm.1, s32[4]{0:T(128)} %valid_ref.1, s32[4]{0:T(128)} %block_ref.1), custom_call_target="tpu_custom_call" | custom-call | tf_op jit(solution)/shard_map/pallas_call | solution.py:250
  31.4 1.9 %copy.9 = bf16[128,2048]{1,0:T(8,128)(2,1)} copy(bf16[128,2048]{1,0:T(8,128)(2,1)} %shard_map.73) | data formatting | bytes 1048576
where the time goes:
time: 33.6 us; the launch traced here: 33.3 us
  Pallas kernels  31.4 us (93%)
  local copies, waits for them, and re-layouts  1.88 us (6%)
    pallas_call x1, Pallas kernels, on_device(): pl.pallas_call(functools.partial(kernel, n, pair, chunk), out_shape=jax.S...  31.4 us
    unnamed x1, local copies, waits for them, and re-layouts  1.88 us

commit v1 on v0

--- a/solution.py
+++ b/solution.py
@@ -18,10 +18,10 @@
 
 def kernel(
     n, pair, chunk,
-    q_hbm, nk_hbm, nv_hbm, ck_hbm, cv_hbm, valid_ref, block_ref,
+    q_hbm, nk_hbm, nv_hbm, ck_hbm, cv_hbm, valid_hbm, block_hbm,
     out_ref,
     kbuf, vbuf, qbuf, numer, stats, code_out, code_in, stat_out, stat_in,
-    cache_bias, span_bias, pad,
+    cache_bias, span_bias, pad, valid_ref, block_ref,
     loc_sem, kv_send, kv_recv, q_send, q_recv, r_send, r_recv, s_send, s_recv,
 ):
     chips = n // pair
@@ -51,7 +51,11 @@
 
     local = [
         pltpu.make_async_copy(sources[i], place(i, 0), loc_sem.at[i]) for i in range(4)
-    ] + [pltpu.make_async_copy(q_hbm, qbuf.at[0], loc_sem.at[4])]
+    ] + [
+        pltpu.make_async_copy(q_hbm, qbuf.at[0], loc_sem.at[4]),
+        pltpu.make_async_copy(valid_hbm, valid_ref, loc_sem.at[5]),
+        pltpu.make_async_copy(block_hbm, block_ref, loc_sem.at[6]),
+    ]
     for copy in local:
         copy.start()
 
@@ -107,6 +111,8 @@
         if c > 0:
             copy.start()
 
+    local[5].wait()
+    local[6].wait()
     key_owner = [me, partner][:pair]
     slot_at = lax.broadcasted_iota(jnp.int32, (8, length), 1)
     for slot in range(pair):
@@ -243,14 +249,19 @@
     heads = cols // DH
     chunk = 4
     chunks = heads // chunk
+    pinned = [
+        pltpu.with_memory_space_constraint(x, pltpu.HBM)
+        for x in (
+            queries, new_keys, new_values, cache_keys, cache_values, valid_len, block_of,
+        )
+    ]
     everywhere = pl.BlockSpec(memory_space=pl.ANY)
-    scalars = pl.BlockSpec(memory_space=pltpu.SMEM)
     dma = pltpu.SemaphoreType.DMA
     keys = pair * (length + rows)
     return pl.pallas_call(
         functools.partial(kernel, n, pair, chunk),
-        out_shape=jax.ShapeDtypeStruct((rows, cols), jnp.bfloat16),
-        in_specs=[everywhere] * 5 + [scalars] * 2,
+        out_shape=pltpu.VMEM((rows, cols), jnp.bfloat16),
+        in_specs=[everywhere] * 7,
         out_specs=pl.BlockSpec(memory_space=pltpu.VMEM),
         scratch_shapes=[
             pltpu.VMEM((keys, kv_cols), jnp.bfloat16),
@@ -265,13 +276,15 @@
             pltpu.VMEM((pair, 8, length), jnp.float32),
             pltpu.VMEM((chips, pair, rows, rows), jnp.float32),
             pltpu.VMEM((3, rows, DH), jnp.float32),
-            dma((5,)), dma((4,)), dma((4,)),
+            pltpu.SMEM(valid_len.shape, jnp.int32),
+            pltpu.SMEM(block_of.shape, jnp.int32),
+            dma((7,)), dma((4,)), dma((4,)),
             dma((chips, chunks)), dma((chips, chunks)),
             dma((chips, chunks)), dma((chips, chunks)),
             dma((chips, chunks)), dma((chips, chunks)),
         ],
-        compiler_params=pltpu.CompilerParams(collective_id=0, has_side_effects=True),
-    )(queries, new_keys, new_values, cache_keys, cache_values, valid_len, block_of)
+        compiler_params=pltpu.CompilerParams(collective_id=0, has_side_effects=True, vmem_limit_bytes=28 * 1024 * 1024),
+    )(*pinned)
 
 
 def solution(mesh):

time: 33.6 us -> 31 us (0.923)
  Pallas kernels: 31.4 us -> 29.9 us
  local copies, waits for them, and re-layouts: 1.88 us -> 0.8 us
    pallas_call x1, Pallas kernels: 31.4 us -> 29.9 us  [on_device(): pl.pallas_call(functools.partial(kernel, n, pair, chunk), out_shape=pltpu...]
    unnamed x1, local copies, waits for them, and re-layouts: 1.88 us -> 0.8 us
where the time goes in v1:
time: 31 us; the launch traced here: 30.7 us
  Pallas kernels  29.9 us (96%)
  local copies, waits for them, and re-layouts  0.8 us (3%)
    pallas_call x1, Pallas kernels, on_device(): pl.pallas_call(functools.partial(kernel, n, pair, chunk), out_shape=pltpu...  29.9 us
    unnamed x1, local copies, waits for them, and re-layouts  0.8 us

profile of v1, /device:TPU:1, one launch (start us, length us, event | category | flops | bytes accessed | tf_op | source)
XLA Modules:
  0.0 30.7 jit_solution(11958479097572905106)
XLA Ops:
  0.0 29.9 %shard_map.73 = bf16[128,2048]{1,0:T(8,128)(2,1)S(1)} custom-call(bf16[128,2048]{1,0:T(8,128)(2,1)} %q_hbm.1, bf16[128,256]{1,0:T(8,128)(2,1)} %nk_hbm.1, bf16[128,256]{1,0:T(8,128)(2,1)} %nv_hbm.1, bf16[1024,256]{1,0:T(8,128)(2,1)} %ck_hbm.1, bf16[1024,256]{1,0:T(8,128)(2,1)} %cv_hbm.1, s32[4]{0:T(128)} %valid_hbm.1, s32[4]{0:T(128)} %block_hbm.1), custom_call_target="tpu_custom_call" | custom-call | tf_op jit(solution)/shard_map/pallas_call | solution.py:261
  29.9 0.8 %copy.9 = bf16[128,2048]{1,0:T(8,128)(2,1)} copy(bf16[128,2048]{1,0:T(8,128)(2,1)S(1)} %shard_map.73) | data formatting | bytes 1048576

commit v2 on v1

v2 whole, which is shorter than its diff:
```python
import functools
import math

import jax
import jax.numpy as jnp
from jax import lax
from jax.experimental import pallas as pl
from jax.experimental.pallas import tpu as pltpu
from jax.sharding import PartitionSpec as P

DH = 128
GROUP = 8
NEGATIVE = -1e30
TO_LOG2 = DH ** (-0.5) * math.log2(math.e)
CODE_MAX = 32767.0
STACK = 2
TILE = 256


def kernel(
    n, pair,
    q_hbm, nk_hbm, nv_hbm, ck_hbm, cv_hbm, valid_hbm, block_hbm,
    out_ref,
    kbuf, vraw, vbuf, qbuf, score_a, score_b, top_a, top_b, own, own_stat,
    code_out, code_in, stat_out, stat_in, span_bias, pad, valid_ref, block_ref,
    loc_sem, kv_send, kv_recv, q_send, q_recv, r_send, r_recv, s_send, s_recv,
):
    chips = n // pair
    rows, cols = q_hbm.shape
    length, kv_cols = ck_hbm.shape
    kv_heads = kv_cols // DH
    heads = cols // DH
    steps = heads // STACK
    width = STACK * DH
    cached = pair * length
    keys = cached + pair * rows
    tiles = [(t, min(TILE, cached - t)) for t in range(0, cached, TILE)]
    tiles += [(cached + t, min(TILE, keys - cached - t)) for t in range(0, keys - cached, TILE)]
    me = lax.axis_index("seq")
    chip, core = me // pair, me % pair
    partner = chip * pair + (pair - 1 - core)

    def ahead(d):
        return ((chip + d) % chips) * pair + (pair - 1 - core)

    def behind(d):
        return ((chip + chips - d) % chips) * pair + (pair - 1 - core)

    sources = (ck_hbm, nk_hbm, cv_hbm, nv_hbm)

    def place(i, slot):
        buf = kbuf if i < 2 else vraw
        start, size = ((slot * length, length), (cached + slot * rows, rows))[i % 2]
        return buf.at[pl.ds(start, size), :]

    local = [
        pltpu.make_async_copy(sources[i], place(i, 0), loc_sem.at[i]) for i in range(4)
    ] + [
        pltpu.make_async_copy(q_hbm, qbuf.at[0], loc_sem.at[4]),
        pltpu.make_async_copy(valid_hbm, valid_ref, loc_sem.at[5]),
        pltpu.make_async_copy(block_hbm, block_ref, loc_sem.at[6]),
    ]
    for i in (4, 5, 6, 0, 1, 2, 3):
        local[i].start()

    barrier = pltpu.get_barrier_semaphore()
    others = [ahead(d) for d in range(1, chips)] + ([partner] if pair > 1 else [])
    for other in others:
        pl.semaphore_signal(barrier, inc=1, device_id={"seq": other})
    pl.semaphore_wait(barrier, len(others))

    def columns(p):
        return pl.ds(pl.multiple_of(p * width, width), width)

    def send_query(d, p):
        return pltpu.make_async_remote_copy(
            src_ref=qbuf.at[0, :, columns(p)],
            dst_ref=qbuf.at[d, :, columns(p)],
            send_sem=q_send.at[d, p], recv_sem=q_recv.at[d, p],
            device_id={"seq": ahead(d)},
        )

    def send_codes(d, p):
        return pltpu.make_async_remote_copy(
            src_ref=code_out.at[d, :, columns(p)],
            dst_ref=code_in.at[d, :, columns(p)],
            send_sem=r_send.at[d, p], recv_sem=r_recv.at[d, p],
            device_id={"seq": behind(d)},
        )

    def send_stats(d, p):
        return pltpu.make_async_remote_copy(
            src_ref=stat_out.at[d, p], dst_ref=stat_in.at[d, p],
            send_sem=s_send.at[d, p], recv_sem=s_recv.at[d, p],
            device_id={"seq": behind(d)},
        )

    kv_copies = []
    if pair > 1:
        kv_copies = [
            pltpu.make_async_remote_copy(
                src_ref=sources[i], dst_ref=place(i, 1),
                send_sem=kv_send.at[i], recv_sem=kv_recv.at[i],
                device_id={"seq": partner},
            )
            for i in range(4)
        ]
    local[4].wait()
    for d in range(1, chips):
        send_query(d, 0).start()
    for copy in kv_copies:
        copy.start()
    for p in range(1, steps):
        for d in range(1, chips):
            send_query(d, p).start()

    local[5].wait()
    local[6].wait()
    key_owner = [me, partner][:pair]
    row_at = lax.broadcasted_iota(jnp.int32, (rows, rows), 0)
    col_at = lax.broadcasted_iota(jnp.int32, (rows, rows), 1)
    for d in range(chips):
        row_pos = block_ref[behind(d) if d else me] * rows + row_at
        for slot in range(pair):
            seen = block_ref[key_owner[slot]] * rows + col_at <= row_pos
            span_bias[d, :, slot * rows : (slot + 1) * rows] = jnp.where(seen, 0.0, NEGATIVE)

    lane = lax.broadcasted_iota(jnp.int32, (rows, DH), 1)
    slot_at = lax.broadcasted_iota(jnp.int32, (TILE, DH), 0)
    ones = jnp.ones((TILE, DH), jnp.bfloat16)

    def live_rows(slot, t):
        live = slot_at + t < valid_ref[key_owner[slot]]
        return jnp.where(live, 1.0, 0.0).astype(jnp.bfloat16)

    def prepare_keys(slot):
        first = kbuf[slot * length : slot * length + 1, :]
        for t in range(0, length, TILE):
            at = pl.ds(slot * length + t, TILE)
            live = live_rows(slot, t)
            for h in range(kv_heads):
                part = pl.ds(h * DH, DH)
                kbuf[at, part] = kbuf[at, part] * live + first[:, h * DH : (h + 1) * DH] * (ones - live)

    def prepare_values(slot):
        for t in range(0, length, TILE):
            at = pl.ds(slot * length + t, TILE)
            live = live_rows(slot, t)
            for h in range(kv_heads):
                vbuf[at, 2 * h * DH : (2 * h + 1) * DH] = vraw[at, h * DH : (h + 1) * DH] * live
                vbuf[at, (2 * h + 1) * DH : (2 * h + 2) * DH] = live
        at = pl.ds(cached + slot * rows, rows)
        for h in range(kv_heads):
            vbuf[at, 2 * h * DH : (2 * h + 1) * DH] = vraw[at, h * DH : (h + 1) * DH]
            vbuf[at, (2 * h + 1) * DH : (2 * h + 2) * DH] = jnp.ones((rows, DH), jnp.bfloat16)

    score = (score_a, score_b)
    peak = (top_a, top_b)

    def find_scores(d, p, buf):
        query = qbuf[d, :, columns(p)]
        stacked = jnp.concatenate([query[:, u * DH : (u + 1) * DH] for u in range(STACK)], axis=0)
        kv_at = pl.ds(pl.multiple_of(p * STACK // GROUP * DH, DH), DH)
        best = None
        for start, size in tiles:
            part = lax.dot_general(
                stacked, kbuf[start : start + size, kv_at], (((1,), (1,)), ((), ())),
                preferred_element_type=jnp.float32,
            )
            if start >= cached:
                bias = span_bias[d, :, start - cached : start - cached + size]
                part = part + jnp.concatenate([bias] * STACK, axis=0)
            score[buf][:, start : start + size] = part
            for c in range(0, size, DH):
                piece = part[:, c : c + DH]
                best = piece if best is None else jnp.maximum(best, piece)
        peak[buf][...] = jnp.broadcast_to(jnp.max(best, axis=1, keepdims=True), peak[buf].shape)

    def attend(p, buf):
        kv_at = pl.ds(pl.multiple_of(p * STACK // GROUP * (2 * DH), 2 * DH), 2 * DH)
        top = peak[buf][...]
        both = None
        for start, size in tiles:
            weights = [
                jnp.exp2((score[buf][:, start + c : start + c + DH] - top) * TO_LOG2).astype(jnp.bfloat16)
                for c in range(0, size, DH)
            ]
            part = jnp.dot(
                jnp.concatenate(weights, axis=1), vbuf[start : start + size, kv_at],
                preferred_element_type=jnp.float32,
            )
            both = part if both is None else both + part
        total = both[:, DH:]
        return both[:, :DH] * (1.0 / total), top * TO_LOG2 + jnp.log2(total)

    def half(x, u):
        return x[u * rows : (u + 1) * rows]

    def finish_own(p, buf):
        value, level = attend(p, buf)
        own[:, columns(p)] = jnp.concatenate([half(value, u) for u in range(STACK)], axis=1)
        levels = half(level, 0)
        for u in range(1, STACK):
            levels = jnp.where(lane == u, half(level, u), levels)
        own_stat[p] = levels

    def finish_other(d, p, buf):
        value, level = attend(p, buf)
        size = jnp.maximum(jnp.max(jnp.abs(value), axis=1, keepdims=True), 1e-30)
        codes = jnp.round(value * (CODE_MAX / size)).astype(jnp.int32).astype(jnp.int16)
        code_out[d, :, columns(p)] = jnp.concatenate([half(codes, u) for u in range(STACK)], axis=1)
        size = jnp.broadcast_to(size * (1.0 / CODE_MAX), level.shape)
        stats = half(level, 0)
        for u in range(1, STACK):
            stats = jnp.where(lane == u, half(level, u), stats)
        for u in range(STACK):
            stats = jnp.where(lane == STACK + u, half(size, u), stats)
        stat_out[d, p] = jnp.transpose(stats)[0 : 2 * STACK]
        send_codes(d, p).start()
        send_stats(d, p).start()

    ping = chips % 2 == 0

    for i in (0, 1):
        local[i].wait()
    prepare_keys(0)
    for copy in kv_copies[:2]:
        copy.wait()
    if pair > 1:
        prepare_keys(1)
    if ping:
        find_scores(0, 0, 0)
    for i in (2, 3):
        local[i].wait()
    prepare_values(0)
    for copy in kv_copies[2:]:
        copy.wait()
    if pair > 1:
        prepare_values(1)

    def body(p, carry):
        for d in range(1, chips):
            send_query(d, p).wait_recv()
        for d in range(chips):
            buf = d % 2
            if not ping:
                find_scores(d, p, buf)
            elif d + 1 < chips:
                find_scores(d + 1, p, 1 - buf)
            else:
                find_scores(0, (p + 1) % steps, 1 - buf)
            if d == 0:
                finish_own(p, buf)
            else:
                finish_other(d, p, buf)
        return carry

    lax.fori_loop(0, steps, body, 0)

    pad[...] = jnp.zeros_like(pad)

    def combine(p, carry):
        mine = own_stat[p]
        top = mine
        got = []
        for d in range(1, chips):
            send_codes(d, p).wait_recv()
            send_stats(d, p).wait_recv()
            pad[0 : 2 * STACK] = stat_in[d, p]
            got.append(jnp.transpose(pad[...]))
            top = jnp.maximum(top, got[-1])
        mine = jnp.exp2(mine - top)
        factors = [jnp.exp2(both - top) for both in got]
        total = mine
        for factor in factors:
            total = total + factor
        inverse = 1.0 / total
        mine = mine * inverse
        factors = [factor * inverse for factor in factors]
        results = []
        for u in range(STACK):
            at = pl.ds(pl.multiple_of((p * STACK + u) * DH, DH), DH)
            result = own[:, at] * mine[:, u : u + 1]
            for d in range(1, chips):
                codes = code_in[d, :, at].astype(jnp.int32).astype(jnp.float32)
                scale = factors[d - 1][:, u : u + 1] * got[d - 1][:, STACK + u : STACK + u + 1]
                result = result + codes * scale
            results.append(result.astype(jnp.bfloat16))
        out_ref[:, columns(p)] = jnp.concatenate(results, axis=1)
        return carry

    lax.fori_loop(0, steps, combine, 0)

    for p in range(steps):
        for d in range(1, chips):
            send_query(d, p).wait_send()
            send_codes(d, p).wait_send()
            send_stats(d, p).wait_send()


def on_device(queries, new_keys, new_values, cache_keys, cache_values, valid_len, block_of):
    n = lax.axis_size("seq")
    pair = 2 if n % 2 == 0 else 1
    chips = n // pair
    rows, cols = queries.shape
    kv_cols = new_keys.shape[1]
    length = cache_keys.shape[0]
    steps = cols // (STACK * DH)
    pinned = [
        pltpu.with_memory_space_constraint(x, pltpu.HBM)
        for x in (
            queries, new_keys, new_values, cache_keys, cache_values, valid_len, block_of,
        )
    ]
    everywhere = pl.BlockSpec(memory_space=pl.ANY)
    dma = pltpu.SemaphoreType.DMA
    keys = pair * (length + rows)
    return pl.pallas_call(
        functools.partial(kernel, n, pair),
        out_shape=pltpu.VMEM((rows, cols), jnp.bfloat16),
        in_specs=[everywhere] * 7,
        out_specs=pl.BlockSpec(memory_space=pltpu.VMEM),
        scratch_shapes=[
            pltpu.VMEM((keys, kv_cols), jnp.bfloat16),
            pltpu.VMEM((keys, kv_cols), jnp.bfloat16),
            pltpu.VMEM((keys, 2 * kv_cols), jnp.bfloat16),
            pltpu.VMEM((chips, rows, cols), jnp.bfloat16),
            pltpu.VMEM((STACK * rows, keys), jnp.float32),
            pltpu.VMEM((STACK * rows, keys), jnp.float32),
            pltpu.VMEM((STACK * rows, DH), jnp.float32),
            pltpu.VMEM((STACK * rows, DH), jnp.float32),
            pltpu.VMEM((rows, cols), jnp.float32),
            pltpu.VMEM((steps, rows, DH), jnp.float32),
            pltpu.VMEM((chips, rows, cols), jnp.int16),
            pltpu.VMEM((chips, rows, cols), jnp.int16),
            pltpu.VMEM((chips, steps, 2 * STACK, rows), jnp.float32),
            pltpu.VMEM((chips, steps, 2 * STACK, rows), jnp.float32),
            pltpu.VMEM((chips, rows, pair * rows), jnp.float32),
            pltpu.VMEM((rows, DH), jnp.float32),
            pltpu.SMEM(valid_len.shape, jnp.int32),
            pltpu.SMEM(block_of.shape, jnp.int32),
            dma((7,)), dma((4,)), dma((4,)),
            dma((chips, steps)), dma((chips, steps)),
            dma((chips, steps)), dma((chips, steps)),
            dma((chips, steps)), dma((chips, steps)),
        ],
        compiler_params=pltpu.CompilerParams(
            collective_id=0, has_side_effects=True, vmem_limit_bytes=48 * 1024 * 1024,
        ),
    )(*pinned)


def solution(mesh):
    placed = (
        P(("groups", "seq"), "head"),
        P(("groups", "seq"), "head"),
        P(("groups", "seq"), "head"),
        P(("groups", "seq"), "head"),
        P(("groups", "seq"), "head"),
        P("groups"),
        P("groups"),
    )
    return jax.shard_map(
        on_device,
        mesh=mesh,
        in_specs=placed,
        out_specs=P(("groups", "seq"), "head"),
        check_vma=False,
    )
```

time: 31 us -> 29.1 us (0.939)
  Pallas kernels: 29.9 us -> 28.2 us
    pallas_call x1, Pallas kernels: 29.9 us -> 28.2 us  [on_device(): pl.pallas_call(functools.partial(kernel, n, pair), out_shape=pltpu.VMEM((...]
where the time goes in v2:
time: 29.1 us; the launch traced here: 29 us
  Pallas kernels  28.2 us (97%)
  local copies, waits for them, and re-layouts  0.8 us (3%)
    pallas_call x1, Pallas kernels, on_device(): pl.pallas_call(functools.partial(kernel, n, pair), out_shape=pltpu.VMEM((...  28.2 us
    unnamed x1, local copies, waits for them, and re-layouts  0.8 us

profile of v2, /device:TPU:1, one launch (start us, length us, event | category | flops | bytes accessed | tf_op | source)
XLA Modules:
  0.0 29.0 jit_solution(7883299209684179290)
XLA Ops:
  0.0 28.2 %shard_map.73 = bf16[128,2048]{1,0:T(8,128)(2,1)S(1)} custom-call(bf16[128,2048]{1,0:T(8,128)(2,1)} %q_hbm.1, bf16[128,256]{1,0:T(8,128)(2,1)} %nk_hbm.1, bf16[128,256]{1,0:T(8,128)(2,1)} %nv_hbm.1, bf16[1024,256]{1,0:T(8,128)(2,1)} %ck_hbm.1, bf16[1024,256]{1,0:T(8,128)(2,1)} %cv_hbm.1, s32[4]{0:T(128)} %valid_hbm.1, s32[4]{0:T(128)} %block_hbm.1), custom_call_target="tpu_custom_call" | custom-call | tf_op jit(solution)/shard_map/pallas_call | solution.py:318
  28.2 0.8 %copy.9 = bf16[128,2048]{1,0:T(8,128)(2,1)} copy(bf16[128,2048]{1,0:T(8,128)(2,1)S(1)} %shard_map.73) | data formatting | bytes 1048576

commit v3 on v2

--- a/solution.py
+++ b/solution.py
@@ -23,7 +23,7 @@
     out_ref,
     kbuf, vraw, vbuf, qbuf, score_a, score_b, top_a, top_b, own, own_stat,
     code_out, code_in, stat_out, stat_in, span_bias, pad, valid_ref, block_ref,
-    loc_sem, kv_send, kv_recv, q_send, q_recv, r_send, r_recv, s_send, s_recv,
+    loc_sem, ql_sem, kv_send, kv_recv, q_send, q_recv, r_send, r_recv, s_send, s_recv,
 ):
     chips = n // pair
     rows, cols = q_hbm.shape
@@ -46,6 +46,17 @@
     def behind(d):
         return ((chip + chips - d) % chips) * pair + (pair - 1 - core)
 
+    barrier = pltpu.get_barrier_semaphore()
+    others = [ahead(d) for d in range(1, chips)] + ([partner] if pair > 1 else [])
+    for other in others:
+        pl.semaphore_signal(barrier, inc=1, device_id={"seq": other})
+
+    def columns(p):
+        return pl.ds(pl.multiple_of(p * width, width), width)
+
+    def local_query(p):
+        return pltpu.make_async_copy(q_hbm.at[:, columns(p)], qbuf.at[0, p], ql_sem.at[p])
+
     sources = (ck_hbm, nk_hbm, cv_hbm, nv_hbm)
 
     def place(i, slot):
@@ -56,34 +67,26 @@
     local = [
         pltpu.make_async_copy(sources[i], place(i, 0), loc_sem.at[i]) for i in range(4)
     ] + [
-        pltpu.make_async_copy(q_hbm, qbuf.at[0], loc_sem.at[4]),
-        pltpu.make_async_copy(valid_hbm, valid_ref, loc_sem.at[5]),
-        pltpu.make_async_copy(block_hbm, block_ref, loc_sem.at[6]),
+                pltpu.make_async_copy(valid_hbm, valid_ref, loc_sem.at[4]),
+        pltpu.make_async_copy(block_hbm, block_ref, loc_sem.at[5]),
     ]
-    for i in (4, 5, 6, 0, 1, 2, 3):
-        local[i].start()
-
-    barrier = pltpu.get_barrier_semaphore()
-    others = [ahead(d) for d in range(1, chips)] + ([partner] if pair > 1 else [])
-    for other in others:
-        pl.semaphore_signal(barrier, inc=1, device_id={"seq": other})
+    for p in range(steps):
+        local_query(p).start()
+    for copy in local:
+        copy.start()
+
     pl.semaphore_wait(barrier, len(others))
-
-    def columns(p):
-        return pl.ds(pl.multiple_of(p * width, width), width)
 
     def send_query(d, p):
         return pltpu.make_async_remote_copy(
-            src_ref=qbuf.at[0, :, columns(p)],
-            dst_ref=qbuf.at[d, :, columns(p)],
+            src_ref=qbuf.at[0, p], dst_ref=qbuf.at[d, p],
             send_sem=q_send.at[d, p], recv_sem=q_recv.at[d, p],
             device_id={"seq": ahead(d)},
         )
 
     def send_codes(d, p):
         return pltpu.make_async_remote_copy(
-            src_ref=code_out.at[d, :, columns(p)],
-            dst_ref=code_in.at[d, :, columns(p)],
+            src_ref=code_out.at[d, p], dst_ref=code_in.at[d, p],
             send_sem=r_send.at[d, p], recv_sem=r_recv.at[d, p],
             device_id={"seq": behind(d)},
         )
@@ -105,17 +108,16 @@
             )
             for i in range(4)
         ]
-    local[4].wait()
-    for d in range(1, chips):
-        send_query(d, 0).start()
-    for copy in kv_copies:
-        copy.start()
-    for p in range(1, steps):
+    for p in range(steps):
+        local_query(p).wait()
         for d in range(1, chips):
             send_query(d, p).start()
-
+        if p == 0:
+            for copy in kv_copies:
+                copy.start()
+
+    local[4].wait()
     local[5].wait()
-    local[6].wait()
     key_owner = [me, partner][:pair]
     row_at = lax.broadcasted_iota(jnp.int32, (rows, rows), 0)
     col_at = lax.broadcasted_iota(jnp.int32, (rows, rows), 1)
@@ -158,7 +160,7 @@
     peak = (top_a, top_b)
 
     def find_scores(d, p, buf):
-        query = qbuf[d, :, columns(p)]
+        query = qbuf[d, p]
         stacked = jnp.concatenate([query[:, u * DH : (u + 1) * DH] for u in range(STACK)], axis=0)
         kv_at = pl.ds(pl.multiple_of(p * STACK // GROUP * DH, DH), DH)
         best = None
@@ -198,7 +200,7 @@
 
     def finish_own(p, buf):
         value, level = attend(p, buf)
-        own[:, columns(p)] = jnp.concatenate([half(value, u) for u in range(STACK)], axis=1)
+        own[p] = jnp.concatenate([half(value, u) for u in range(STACK)], axis=1)
         levels = half(level, 0)
         for u in range(1, STACK):
             levels = jnp.where(lane == u, half(level, u), levels)
@@ -206,16 +208,20 @@
 
     def finish_other(d, p, buf):
         value, level = attend(p, buf)
-        size = jnp.maximum(jnp.max(jnp.abs(value), axis=1, keepdims=True), 1e-30)
-        codes = jnp.round(value * (CODE_MAX / size)).astype(jnp.int32).astype(jnp.int16)
-        code_out[d, :, columns(p)] = jnp.concatenate([half(codes, u) for u in range(STACK)], axis=1)
-        size = jnp.broadcast_to(size * (1.0 / CODE_MAX), level.shape)
-        stats = half(level, 0)
+        size = jnp.abs(half(value, 0))
         for u in range(1, STACK):
+            size = jnp.maximum(size, jnp.abs(half(value, u)))
+        size = jnp.maximum(jnp.max(size, axis=1, keepdims=True), 1e-30)
+        scale = CODE_MAX / size
+        codes = [
+            jnp.round(half(value, u) * scale).astype(jnp.int32).astype(jnp.int16)
+            for u in range(STACK)
+        ]
+        code_out[d, p] = jnp.concatenate(codes, axis=1)
+        stats = size * (1.0 / CODE_MAX)
+        for u in range(STACK):
             stats = jnp.where(lane == u, half(level, u), stats)
-        for u in range(STACK):
-            stats = jnp.where(lane == STACK + u, half(size, u), stats)
-        stat_out[d, p] = jnp.transpose(stats)[0 : 2 * STACK]
+        stat_out[d, p] = jnp.transpose(stats)[0 : STACK + 1]
         send_codes(d, p).start()
         send_stats(d, p).start()
 
@@ -266,7 +272,7 @@
         for d in range(1, chips):
             send_codes(d, p).wait_recv()
             send_stats(d, p).wait_recv()
-            pad[0 : 2 * STACK] = stat_in[d, p]
+            pad[0 : STACK + 1] = stat_in[d, p]
             got.append(jnp.transpose(pad[...]))
             top = jnp.maximum(top, got[-1])
         mine = jnp.exp2(mine - top)
@@ -279,11 +285,11 @@
         factors = [factor * inverse for factor in factors]
         results = []
         for u in range(STACK):
-            at = pl.ds(pl.multiple_of((p * STACK + u) * DH, DH), DH)
-            result = own[:, at] * mine[:, u : u + 1]
+            at = pl.ds(u * DH, DH)
+            result = own[p, :, at] * mine[:, u : u + 1]
             for d in range(1, chips):
-                codes = code_in[d, :, at].astype(jnp.int32).astype(jnp.float32)
-                scale = factors[d - 1][:, u : u + 1] * got[d - 1][:, STACK + u : STACK + u + 1]
+                codes = code_in[d, p, :, at].astype(jnp.int32).astype(jnp.float32)
+                scale = factors[d - 1][:, u : u + 1] * got[d - 1][:, STACK : STACK + 1]
                 result = result + codes * scale
             results.append(result.astype(jnp.bfloat16))
         out_ref[:, columns(p)] = jnp.concatenate(results, axis=1)
@@ -324,22 +330,22 @@
             pltpu.VMEM((keys, kv_cols), jnp.bfloat16),
             pltpu.VMEM((keys, kv_cols), jnp.bfloat16),
             pltpu.VMEM((keys, 2 * kv_cols), jnp.bfloat16),
-            pltpu.VMEM((chips, rows, cols), jnp.bfloat16),
+            pltpu.VMEM((chips, steps, rows, STACK * DH), jnp.bfloat16),
             pltpu.VMEM((STACK * rows, keys), jnp.float32),
             pltpu.VMEM((STACK * rows, keys), jnp.float32),
             pltpu.VMEM((STACK * rows, DH), jnp.float32),
             pltpu.VMEM((STACK * rows, DH), jnp.float32),
-            pltpu.VMEM((rows, cols), jnp.float32),
+            pltpu.VMEM((steps, rows, STACK * DH), jnp.float32),
             pltpu.VMEM((steps, rows, DH), jnp.float32),
-            pltpu.VMEM((chips, rows, cols), jnp.int16),
-            pltpu.VMEM((chips, rows, cols), jnp.int16),
-            pltpu.VMEM((chips, steps, 2 * STACK, rows), jnp.float32),
-            pltpu.VMEM((chips, steps, 2 * STACK, rows), jnp.float32),
+            pltpu.VMEM((chips, steps, rows, STACK * DH), jnp.int16),
+            pltpu.VMEM((chips, steps, rows, STACK * DH), jnp.int16),
+            pltpu.VMEM((chips, steps, STACK + 1, rows), jnp.float32),
+            pltpu.VMEM((chips, steps, STACK + 1, rows), jnp.float32),
             pltpu.VMEM((chips, rows, pair * rows), jnp.float32),
             pltpu.VMEM((rows, DH), jnp.float32),
             pltpu.SMEM(valid_len.shape, jnp.int32),
             pltpu.SMEM(block_of.shape, jnp.int32),
-            dma((7,)), dma((4,)), dma((4,)),
+            dma((6,)), dma((steps,)), dma((4,)), dma((4,)),
             dma((chips, steps)), dma((chips, steps)),
             dma((chips, steps)), dma((chips, steps)),
             dma((chips, steps)), dma((chips, steps)),

time: 29.1 us -> 28.9 us (level)
  no operation moved by 1% of the time
where the time goes in v3:
time: 28.9 us; the launch traced here: 28.8 us
  Pallas kernels  28 us (97%)
  local copies, waits for them, and re-layouts  0.8 us (3%)
    pallas_call x1, Pallas kernels, on_device(): pl.pallas_call(functools.partial(kernel, n, pair), out_shape=pltpu.VMEM((...  28 us
    unnamed x1, local copies, waits for them, and re-layouts  0.8 us

profile of v3, /device:TPU:1, one launch (start us, length us, event | category | flops | bytes accessed | tf_op | source)
XLA Modules:
  0.0 28.8 jit_solution(4184642079981882107)
XLA Ops:
  0.0 28.0 %shard_map.73 = bf16[128,2048]{1,0:T(8,128)(2,1)S(1)} custom-call(bf16[128,2048]{1,0:T(8,128)(2,1)} %q_hbm.1, bf16[128,256]{1,0:T(8,128)(2,1)} %nk_hbm.1, bf16[128,256]{1,0:T(8,128)(2,1)} %nv_hbm.1, bf16[1024,256]{1,0:T(8,128)(2,1)} %ck_hbm.1, bf16[1024,256]{1,0:T(8,128)(2,1)} %cv_hbm.1, s32[4]{0:T(128)} %valid_hbm.1, s32[4]{0:T(128)} %block_hbm.1), custom_call_target="tpu_custom_call" | custom-call | tf_op jit(solution)/shard_map/pallas_call | solution.py:324
  28.0 0.8 %copy.9 = bf16[128,2048]{1,0:T(8,128)(2,1)} copy(bf16[128,2048]{1,0:T(8,128)(2,1)S(1)} %shard_map.73) | data formatting | bytes 1048576

commit v4 on v3

--- a/solution.py
+++ b/solution.py
@@ -222,8 +222,8 @@
         for u in range(STACK):
             stats = jnp.where(lane == u, half(level, u), stats)
         stat_out[d, p] = jnp.transpose(stats)[0 : STACK + 1]
+        send_stats(d, p).start()
         send_codes(d, p).start()
-        send_stats(d, p).start()
 
     ping = chips % 2 == 0
 
@@ -270,7 +270,6 @@
         top = mine
         got = []
         for d in range(1, chips):
-            send_codes(d, p).wait_recv()
             send_stats(d, p).wait_recv()
             pad[0 : STACK + 1] = stat_in[d, p]
             got.append(jnp.transpose(pad[...]))
@@ -283,15 +282,17 @@
         inverse = 1.0 / total
         mine = mine * inverse
         factors = [factor * inverse for factor in factors]
-        results = []
-        for u in range(STACK):
-            at = pl.ds(u * DH, DH)
-            result = own[p, :, at] * mine[:, u : u + 1]
-            for d in range(1, chips):
-                codes = code_in[d, p, :, at].astype(jnp.int32).astype(jnp.float32)
-                scale = factors[d - 1][:, u : u + 1] * got[d - 1][:, STACK : STACK + 1]
-                result = result + codes * scale
-            results.append(result.astype(jnp.bfloat16))
+        scales = [
+            [factors[d - 1][:, u : u + 1] * got[d - 1][:, STACK : STACK + 1] for d in range(1, chips)]
+            for u in range(STACK)
+        ]
+        results = [own[p, :, u * DH : (u + 1) * DH] * mine[:, u : u + 1] for u in range(STACK)]
+        for d in range(1, chips):
+            send_codes(d, p).wait_recv()
+            for u in range(STACK):
+                codes = code_in[d, p, :, u * DH : (u + 1) * DH].astype(jnp.int32).astype(jnp.float32)
+                results[u] = results[u] + codes * scales[u][d - 1]
+        results = [result.astype(jnp.bfloat16) for result in results]
         out_ref[:, columns(p)] = jnp.concatenate(results, axis=1)
         return carry
 

time: 28.9 us -> 28.7 us (level)
  no operation moved by 1% of the time
where the time goes in v4:
time: 28.7 us; the launch traced here: 28.6 us
  Pallas kernels  27.8 us (97%)
  local copies, waits for them, and re-layouts  0.8 us (3%)
    pallas_call x1, Pallas kernels, on_device(): pl.pallas_call(functools.partial(kernel, n, pair), out_shape=pltpu.VMEM((...  27.8 us
    unnamed x1, local copies, waits for them, and re-layouts  0.8 us

profile of v4, /device:TPU:1, one launch (start us, length us, event | category | flops | bytes accessed | tf_op | source)
XLA Modules:
  0.0 28.6 jit_solution(8445888218125676784)
XLA Ops:
  0.0 27.8 %shard_map.73 = bf16[128,2048]{1,0:T(8,128)(2,1)S(1)} custom-call(bf16[128,2048]{1,0:T(8,128)(2,1)} %q_hbm.1, bf16[128,256]{1,0:T(8,128)(2,1)} %nk_hbm.1, bf16[128,256]{1,0:T(8,128)(2,1)} %nv_hbm.1, bf16[1024,256]{1,0:T(8,128)(2,1)} %ck_hbm.1, bf16[1024,256]{1,0:T(8,128)(2,1)} %cv_hbm.1, s32[4]{0:T(128)} %valid_hbm.1, s32[4]{0:T(128)} %block_hbm.1), custom_call_target="tpu_custom_call" | custom-call | tf_op jit(solution)/shard_map/pallas_call | solution.py:325
  27.8 0.8 %copy.9 = bf16[128,2048]{1,0:T(8,128)(2,1)} copy(bf16[128,2048]{1,0:T(8,128)(2,1)S(1)} %shard_map.73) | data formatting | bytes 1048576

commit v5 on v4

--- a/solution.py
+++ b/solution.py
@@ -22,7 +22,7 @@
     q_hbm, nk_hbm, nv_hbm, ck_hbm, cv_hbm, valid_hbm, block_hbm,
     out_ref,
     kbuf, vraw, vbuf, qbuf, score_a, score_b, top_a, top_b, own, own_stat,
-    code_out, code_in, stat_out, stat_in, span_bias, pad, valid_ref, block_ref,
+    code_out, code_in, stat_out, stat_in, span_bias, repeat, pad, valid_ref, block_ref,
     loc_sem, ql_sem, kv_send, kv_recv, q_send, q_recv, r_send, r_recv, s_send, s_recv,
 ):
     chips = n // pair
@@ -155,6 +155,10 @@
         for h in range(kv_heads):
             vbuf[at, 2 * h * DH : (2 * h + 1) * DH] = vraw[at, h * DH : (h + 1) * DH]
             vbuf[at, (2 * h + 1) * DH : (2 * h + 2) * DH] = jnp.ones((rows, DH), jnp.bfloat16)
+
+    for slot in range(pair):
+        copies = (length - valid_ref[key_owner[slot]]).astype(jnp.float32)
+        repeat[slot] = jnp.where(lane[0:8] == 0, 1.0 - copies, 1.0)
 
     score = (score_a, score_b)
     peak = (top_a, top_b)
@@ -181,19 +185,22 @@
     def attend(p, buf):
         kv_at = pl.ds(pl.multiple_of(p * STACK // GROUP * (2 * DH), 2 * DH), 2 * DH)
         top = peak[buf][...]
-        both = None
+        value = total = None
         for start, size in tiles:
-            weights = [
-                jnp.exp2((score[buf][:, start + c : start + c + DH] - top) * TO_LOG2).astype(jnp.bfloat16)
-                for c in range(0, size, DH)
-            ]
+            rounded = []
+            for c in range(start, start + size, DH):
+                weights = jnp.exp2((score[buf][:, c : c + DH] - top) * TO_LOG2)
+                rounded.append(weights.astype(jnp.bfloat16))
+                if c < cached and c % length == 0:
+                    weights = weights * repeat[c // length, 0:1]
+                total = weights if total is None else total + weights
             part = jnp.dot(
-                jnp.concatenate(weights, axis=1), vbuf[start : start + size, kv_at],
+                jnp.concatenate(rounded, axis=1), vbuf[start : start + size, kv_at],
                 preferred_element_type=jnp.float32,
             )
-            both = part if both is None else both + part
-        total = both[:, DH:]
-        return both[:, :DH] * (1.0 / total), top * TO_LOG2 + jnp.log2(total)
+            value = part if value is None else value + part
+        total = jnp.sum(total, axis=1, keepdims=True)
+        return value[:, :DH] * (1.0 / total), top * TO_LOG2 + jnp.log2(total)
 
     def half(x, u):
         return x[u * rows : (u + 1) * rows]
@@ -343,6 +350,7 @@
             pltpu.VMEM((chips, steps, STACK + 1, rows), jnp.float32),
             pltpu.VMEM((chips, steps, STACK + 1, rows), jnp.float32),
             pltpu.VMEM((chips, rows, pair * rows), jnp.float32),
+            pltpu.VMEM((pair, 8, DH), jnp.float32),
             pltpu.VMEM((rows, DH), jnp.float32),
             pltpu.SMEM(valid_len.shape, jnp.int32),
             pltpu.SMEM(block_of.shape, jnp.int32),

time: 28.7 us -> 28.7 us (level)
  no operation moved by 1% of the time
where the time goes in v5:
time: 28.7 us; the launch traced here: 28.6 us
  Pallas kernels  27.8 us (97%)
  local copies, waits for them, and re-layouts  0.8 us (3%)
    pallas_call x1, Pallas kernels, on_device(): pl.pallas_call(functools.partial(kernel, n, pair), out_shape=pltpu.VMEM((...  27.8 us
    unnamed x1, local copies, waits for them, and re-layouts  0.8 us

profile of v5, /device:TPU:1, one launch (start us, length us, event | category | flops | bytes accessed | tf_op | source)
XLA Modules:
  0.0 28.6 jit_solution(7920645246257677160)
XLA Ops:
  0.0 27.8 %shard_map.73 = bf16[128,2048]{1,0:T(8,128)(2,1)S(1)} custom-call(bf16[128,2048]{1,0:T(8,128)(2,1)} %q_hbm.1, bf16[128,256]{1,0:T(8,128)(2,1)} %nk_hbm.1, bf16[128,256]{1,0:T(8,128)(2,1)} %nv_hbm.1, bf16[1024,256]{1,0:T(8,128)(2,1)} %ck_hbm.1, bf16[1024,256]{1,0:T(8,128)(2,1)} %cv_hbm.1, s32[4]{0:T(128)} %valid_hbm.1, s32[4]{0:T(128)} %block_hbm.1), custom_call_target="tpu_custom_call" | custom-call | tf_op jit(solution)/shard_map/pallas_call | solution.py:332
  27.8 0.8 %copy.9 = bf16[128,2048]{1,0:T(8,128)(2,1)} copy(bf16[128,2048]{1,0:T(8,128)(2,1)S(1)} %shard_map.73) | data formatting | bytes 1048576

commit v6 on v5

--- a/solution.py
+++ b/solution.py
@@ -55,7 +55,10 @@
         return pl.ds(pl.multiple_of(p * width, width), width)
 
     def local_query(p):
-        return pltpu.make_async_copy(q_hbm.at[:, columns(p)], qbuf.at[0, p], ql_sem.at[p])
+        return pltpu.make_async_copy(q_hbm.at[:, columns(p)], qbuf.at[0, p], ql_sem.at[min(p, 1)])
+
+    def await_bytes(ref, sem):
+        pltpu.make_async_copy(ref, ref, sem).wait()
 
     sources = (ck_hbm, nk_hbm, cv_hbm, nv_hbm)
 
@@ -65,10 +68,10 @@
         return buf.at[pl.ds(start, size), :]
 
     local = [
-        pltpu.make_async_copy(sources[i], place(i, 0), loc_sem.at[i]) for i in range(4)
+        pltpu.make_async_copy(sources[i], place(i, 0), loc_sem.at[i // 2]) for i in range(4)
     ] + [
-                pltpu.make_async_copy(valid_hbm, valid_ref, loc_sem.at[4]),
-        pltpu.make_async_copy(block_hbm, block_ref, loc_sem.at[5]),
+        pltpu.make_async_copy(valid_hbm, valid_ref, loc_sem.at[2]),
+        pltpu.make_async_copy(block_hbm, block_ref, loc_sem.at[3]),
     ]
     for p in range(steps):
         local_query(p).start()
@@ -77,24 +80,27 @@
 
     pl.semaphore_wait(barrier, len(others))
 
-    def send_query(d, p):
+    def send_query(d, p, count=1):
         return pltpu.make_async_remote_copy(
-            src_ref=qbuf.at[0, p], dst_ref=qbuf.at[d, p],
-            send_sem=q_send.at[d, p], recv_sem=q_recv.at[d, p],
+            src_ref=qbuf.at[0, pl.ds(p, count)], dst_ref=qbuf.at[d, pl.ds(p, count)],
+            send_sem=q_send.at[d - 1], recv_sem=q_recv.at[d - 1, p // 2 + 1 if count == 2 else p],
             device_id={"seq": ahead(d)},
         )
 
-    def send_codes(d, p):
+    def code_slot(p, count):
+        return {1: p - (steps - 2) // 2, 2: p // 2}.get(count, 0)
+
+    def send_codes(d, p, count=1):
         return pltpu.make_async_remote_copy(
-            src_ref=code_out.at[d, p], dst_ref=code_in.at[d, p],
-            send_sem=r_send.at[d, p], recv_sem=r_recv.at[d, p],
+            src_ref=code_out.at[d, pl.ds(p, count)], dst_ref=code_in.at[d, pl.ds(p, count)],
+            send_sem=r_send.at[d - 1], recv_sem=r_recv.at[d - 1, code_slot(p, count)],
             device_id={"seq": behind(d)},
         )
 
-    def send_stats(d, p):
+    def send_stats(d, p, count=1):
         return pltpu.make_async_remote_copy(
-            src_ref=stat_out.at[d, p], dst_ref=stat_in.at[d, p],
-            send_sem=s_send.at[d, p], recv_sem=s_recv.at[d, p],
+            src_ref=stat_out.at[d, pl.ds(p, count)], dst_ref=stat_in.at[d, pl.ds(p, count)],
+            send_sem=s_send.at[d - 1], recv_sem=s_recv.at[d - 1, code_slot(p, count)],
             device_id={"seq": behind(d)},
         )
 
@@ -103,18 +109,20 @@
         kv_copies = [
             pltpu.make_async_remote_copy(
                 src_ref=sources[i], dst_ref=place(i, 1),
-                send_sem=kv_send.at[i], recv_sem=kv_recv.at[i],
+                send_sem=kv_send.at[0], recv_sem=kv_recv.at[i // 2],
                 device_id={"seq": partner},
             )
             for i in range(4)
         ]
-    for p in range(steps):
-        local_query(p).wait()
+    local_query(0).wait()
+    for d in range(1, chips):
+        send_query(d, 0).start()
+    for copy in kv_copies:
+        copy.start()
+    await_bytes(qbuf.at[0, pl.ds(1, steps - 1)], ql_sem.at[1])
+    for first, count in [(1, 1)] + [(p, 2) for p in range(2, steps, 2)]:
         for d in range(1, chips):
-            send_query(d, p).start()
-        if p == 0:
-            for copy in kv_copies:
-                copy.start()
+            send_query(d, first, count).start()
 
     local[4].wait()
     local[5].wait()
@@ -229,31 +237,45 @@
         for u in range(STACK):
             stats = jnp.where(lane == u, half(level, u), stats)
         stat_out[d, p] = jnp.transpose(stats)[0 : STACK + 1]
-        send_stats(d, p).start()
-        send_codes(d, p).start()
+
+        @pl.when(p >= steps - 2)
+        def _():
+            send_stats(d, p).start()
+            send_codes(d, p).start()
+
+        @pl.when((p < steps - 2) & (p % 2 == 1))
+        def _():
+            send_stats(d, p - 1, 2).start()
+            send_codes(d, p - 1, 2).start()
 
     ping = chips % 2 == 0
 
-    for i in (0, 1):
-        local[i].wait()
+    share = pl.ds(0, length + rows)
+    await_bytes(kbuf.at[share], loc_sem.at[0])
     prepare_keys(0)
-    for copy in kv_copies[:2]:
-        copy.wait()
     if pair > 1:
+        await_bytes(kbuf.at[share], kv_recv.at[0])
         prepare_keys(1)
     if ping:
         find_scores(0, 0, 0)
-    for i in (2, 3):
-        local[i].wait()
+    await_bytes(vraw.at[share], loc_sem.at[1])
     prepare_values(0)
-    for copy in kv_copies[2:]:
-        copy.wait()
     if pair > 1:
+        await_bytes(vraw.at[share], kv_recv.at[1])
         prepare_values(1)
+        await_bytes(kbuf, kv_send.at[0])
 
     def body(p, carry):
-        for d in range(1, chips):
-            send_query(d, p).wait_recv()
+        @pl.when(p < 2)
+        def _():
+            for d in range(1, chips):
+                send_query(d, p).wait_recv()
+
+        @pl.when((p >= 2) & (p % 2 == 0))
+        def _():
+            for d in range(1, chips):
+                send_query(d, p, 2).wait_recv()
+
         for d in range(chips):
             buf = d % 2
             if not ping:
@@ -272,12 +294,21 @@
 
     pad[...] = jnp.zeros_like(pad)
 
+    def await_group(send, d, p):
+        @pl.when(p >= steps - 2)
+        def _():
+            send(d, p).wait_recv()
+
+        @pl.when((p < steps - 2) & (p % 2 == 0))
+        def _():
+            send(d, p, 2).wait_recv()
+
     def combine(p, carry):
         mine = own_stat[p]
         top = mine
         got = []
         for d in range(1, chips):
-            send_stats(d, p).wait_recv()
+            await_group(send_stats, d, p)
             pad[0 : STACK + 1] = stat_in[d, p]
             got.append(jnp.transpose(pad[...]))
             top = jnp.maximum(top, got[-1])
@@ -295,7 +326,7 @@
         ]
         results = [own[p, :, u * DH : (u + 1) * DH] * mine[:, u : u + 1] for u in range(STACK)]
         for d in range(1, chips):
-            send_codes(d, p).wait_recv()
+            await_group(send_codes, d, p)
             for u in range(STACK):
                 codes = code_in[d, p, :, u * DH : (u + 1) * DH].astype(jnp.int32).astype(jnp.float32)
                 results[u] = results[u] + codes * scales[u][d - 1]
@@ -305,11 +336,10 @@
 
     lax.fori_loop(0, steps, combine, 0)
 
-    for p in range(steps):
-        for d in range(1, chips):
-            send_query(d, p).wait_send()
-            send_codes(d, p).wait_send()
-            send_stats(d, p).wait_send()
+    for d in range(1, chips):
+        send_query(d, 0, steps).wait_send()
+        send_codes(d, 0, steps).wait_send()
+        send_stats(d, 0, steps).wait_send()
 
 
 def on_device(queries, new_keys, new_values, cache_keys, cache_values, valid_len, block_of):
@@ -320,6 +350,7 @@
     kv_cols = new_keys.shape[1]
     length = cache_keys.shape[0]
     steps = cols // (STACK * DH)
+    links = max(1, chips - 1)
     pinned = [
         pltpu.with_memory_space_constraint(x, pltpu.HBM)
         for x in (
@@ -354,10 +385,10 @@
             pltpu.VMEM((rows, DH), jnp.float32),
             pltpu.SMEM(valid_len.shape, jnp.int32),
             pltpu.SMEM(block_of.shape, jnp.int32),
-            dma((6,)), dma((steps,)), dma((4,)), dma((4,)),
-            dma((chips, steps)), dma((chips, steps)),
-            dma((chips, steps)), dma((chips, steps)),
-            dma((chips, steps)), dma((chips, steps)),
+            dma((4,)), dma((2,)), dma((1,)), dma((2,)),
+            dma((links,)), dma((links, steps // 2 + 1)),
+            dma((links,)), dma((links, steps // 2 + 1)),
+            dma((links,)), dma((links, steps // 2 + 1)),
         ],
         compiler_params=pltpu.CompilerParams(
             collective_id=0, has_side_effects=True, vmem_limit_bytes=48 * 1024 * 1024,

time: 28.7 us -> 27.9 us (0.972)
  Pallas kernels: 27.8 us -> 26.9 us
    pallas_call x1, Pallas kernels: 27.8 us -> 26.9 us  [on_device(): pl.pallas_call(functools.partial(kernel, n, pair), out_shape=pltpu.VMEM((...]
where the time goes in v6:
time: 27.9 us; the launch traced here: 27.7 us
  Pallas kernels  26.9 us (96%)
  local copies, waits for them, and re-layouts  0.8 us (3%)
    pallas_call x1, Pallas kernels, on_device(): pl.pallas_call(functools.partial(kernel, n, pair), out_shape=pltpu.VMEM((...  26.9 us
    unnamed x1, local copies, waits for them, and re-layouts  0.8 us

profile of v6, /device:TPU:1, one launch (start us, length us, event | category | flops | bytes accessed | tf_op | source)
XLA Modules:
  0.0 27.7 jit_solution(14642928147291326703)
XLA Ops:
  0.0 26.9 %shard_map.73 = bf16[128,2048]{1,0:T(8,128)(2,1)S(1)} custom-call(bf16[128,2048]{1,0:T(8,128)(2,1)} %q_hbm.1, bf16[128,256]{1,0:T(8,128)(2,1)} %nk_hbm.1, bf16[128,256]{1,0:T(8,128)(2,1)} %nv_hbm.1, bf16[1024,256]{1,0:T(8,128)(2,1)} %ck_hbm.1, bf16[1024,256]{1,0:T(8,128)(2,1)} %cv_hbm.1, s32[4]{0:T(128)} %valid_hbm.1, s32[4]{0:T(128)} %block_hbm.1), custom_call_target="tpu_custom_call" | custom-call | tf_op jit(solution)/shard_map/pallas_call | solution.py:363
  26.9 0.8 %copy.9 = bf16[128,2048]{1,0:T(8,128)(2,1)} copy(bf16[128,2048]{1,0:T(8,128)(2,1)S(1)} %shard_map.73) | data formatting | bytes 1048576

commit v7 on v6

--- a/solution.py
+++ b/solution.py
@@ -68,10 +68,10 @@
         return buf.at[pl.ds(start, size), :]
 
     local = [
-        pltpu.make_async_copy(sources[i], place(i, 0), loc_sem.at[i // 2]) for i in range(4)
+        pltpu.make_async_copy(sources[i], place(i, 0), loc_sem.at[0]) for i in range(4)
     ] + [
-        pltpu.make_async_copy(valid_hbm, valid_ref, loc_sem.at[2]),
-        pltpu.make_async_copy(block_hbm, block_ref, loc_sem.at[3]),
+        pltpu.make_async_copy(valid_hbm, valid_ref, loc_sem.at[1]),
+        pltpu.make_async_copy(block_hbm, block_ref, loc_sem.at[2]),
     ]
     for p in range(steps):
         local_query(p).start()
@@ -100,7 +100,7 @@
     def send_stats(d, p, count=1):
         return pltpu.make_async_remote_copy(
             src_ref=stat_out.at[d, pl.ds(p, count)], dst_ref=stat_in.at[d, pl.ds(p, count)],
-            send_sem=s_send.at[d - 1], recv_sem=s_recv.at[d - 1, code_slot(p, count)],
+            send_sem=s_send.at[d - 1], recv_sem=s_recv.at[d - 1, p - (steps - 3) if count == 1 else 0],
             device_id={"seq": behind(d)},
         )
 
@@ -109,7 +109,7 @@
         kv_copies = [
             pltpu.make_async_remote_copy(
                 src_ref=sources[i], dst_ref=place(i, 1),
-                send_sem=kv_send.at[0], recv_sem=kv_recv.at[i // 2],
+                send_sem=kv_send.at[0], recv_sem=kv_recv.at[0],
                 device_id={"seq": partner},
             )
             for i in range(4)
@@ -245,25 +245,23 @@
 
         @pl.when((p < steps - 2) & (p % 2 == 1))
         def _():
-            send_stats(d, p - 1, 2).start()
+            @pl.when(p == steps - 3)
+            def _():
+                send_stats(d, 0, steps - 2).start()
+
             send_codes(d, p - 1, 2).start()
 
     ping = chips % 2 == 0
 
-    share = pl.ds(0, length + rows)
-    await_bytes(kbuf.at[share], loc_sem.at[0])
+    await_bytes(kbuf if pair > 1 else vbuf, loc_sem.at[0])
     prepare_keys(0)
     if pair > 1:
-        await_bytes(kbuf.at[share], kv_recv.at[0])
+        await_bytes(kbuf, kv_recv.at[0])
         prepare_keys(1)
     if ping:
         find_scores(0, 0, 0)
-    await_bytes(vraw.at[share], loc_sem.at[1])
-    prepare_values(0)
-    if pair > 1:
-        await_bytes(vraw.at[share], kv_recv.at[1])
-        prepare_values(1)
-        await_bytes(kbuf, kv_send.at[0])
+    for slot in range(pair):
+        prepare_values(slot)
 
     def body(p, carry):
         @pl.when(p < 2)
@@ -294,21 +292,28 @@
 
     pad[...] = jnp.zeros_like(pad)
 
-    def await_group(send, d, p):
+    def await_codes(d, p):
         @pl.when(p >= steps - 2)
         def _():
-            send(d, p).wait_recv()
+            send_codes(d, p).wait_recv()
 
         @pl.when((p < steps - 2) & (p % 2 == 0))
         def _():
-            send(d, p, 2).wait_recv()
+            send_codes(d, p, 2).wait_recv()
 
     def combine(p, carry):
         mine = own_stat[p]
         top = mine
         got = []
         for d in range(1, chips):
-            await_group(send_stats, d, p)
+            @pl.when(p >= steps - 2)
+            def _():
+                send_stats(d, p).wait_recv()
+
+            @pl.when(p == 0)
+            def _():
+                send_stats(d, 0, steps - 2).wait_recv()
+
             pad[0 : STACK + 1] = stat_in[d, p]
             got.append(jnp.transpose(pad[...]))
             top = jnp.maximum(top, got[-1])
@@ -326,7 +331,7 @@
         ]
         results = [own[p, :, u * DH : (u + 1) * DH] * mine[:, u : u + 1] for u in range(STACK)]
         for d in range(1, chips):
-            await_group(send_codes, d, p)
+            await_codes(d, p)
             for u in range(STACK):
                 codes = code_in[d, p, :, u * DH : (u + 1) * DH].astype(jnp.int32).astype(jnp.float32)
                 results[u] = results[u] + codes * scales[u][d - 1]
@@ -336,6 +341,8 @@
 
     lax.fori_loop(0, steps, combine, 0)
 
+    if pair > 1:
+        await_bytes(kbuf, kv_send.at[0])
     for d in range(1, chips):
         send_query(d, 0, steps).wait_send()
         send_codes(d, 0, steps).wait_send()
@@ -385,10 +392,10 @@
             pltpu.VMEM((rows, DH), jnp.float32),
             pltpu.SMEM(valid_len.shape, jnp.int32),
             pltpu.SMEM(block_of.shape, jnp.int32),
-            dma((4,)), dma((2,)), dma((1,)), dma((2,)),
+            dma((3,)), dma((2,)), dma((1,)), dma((1,)),
             dma((links,)), dma((links, steps // 2 + 1)),
             dma((links,)), dma((links, steps // 2 + 1)),
-            dma((links,)), dma((links, steps // 2 + 1)),
+            dma((links,)), dma((links, 3)),
         ],
         compiler_params=pltpu.CompilerParams(
             collective_id=0, has_side_effects=True, vmem_limit_bytes=48 * 1024 * 1024,

time: 27.9 us -> 28 us (level)
  no operation moved by 1% of the time
where the time goes in v7:
time: 28 us; the launch traced here: 27.7 us
  Pallas kernels  26.9 us (96%)
  local copies, waits for them, and re-layouts  0.8 us (3%)
    pallas_call x1, Pallas kernels, on_device(): pl.pallas_call(functools.partial(kernel, n, pair), out_shape=pltpu.VMEM((...  26.9 us
    unnamed x1, local copies, waits for them, and re-layouts  0.8 us

profile of v7, /device:TPU:1, one launch (start us, length us, event | category | flops | bytes accessed | tf_op | source)
XLA Modules:
  0.0 27.7 jit_solution(1645575535924163055)
XLA Ops:
  0.0 26.9 %shard_map.73 = bf16[128,2048]{1,0:T(8,128)(2,1)S(1)} custom-call(bf16[128,2048]{1,0:T(8,128)(2,1)} %q_hbm.1, bf16[128,256]{1,0:T(8,128)(2,1)} %nk_hbm.1, bf16[128,256]{1,0:T(8,128)(2,1)} %nv_hbm.1, bf16[1024,256]{1,0:T(8,128)(2,1)} %ck_hbm.1, bf16[1024,256]{1,0:T(8,128)(2,1)} %cv_hbm.1, s32[4]{0:T(128)} %valid_hbm.1, s32[4]{0:T(128)} %block_hbm.1), custom_call_target="tpu_custom_call" | custom-call | tf_op jit(solution)/shard_map/pallas_call | solution.py:370
  26.9 0.8 %copy.9 = bf16[128,2048]{1,0:T(8,128)(2,1)} copy(bf16[128,2048]{1,0:T(8,128)(2,1)S(1)} %shard_map.73) | data formatting | bytes 1048576

commit v8 on v6

--- a/solution.py
+++ b/solution.py
@@ -75,8 +75,8 @@
     ]
     for p in range(steps):
         local_query(p).start()
-    for copy in local:
-        copy.start()
+    local[4].start()
+    local[5].start()
 
     pl.semaphore_wait(barrier, len(others))
 
@@ -118,6 +118,8 @@
     for d in range(1, chips):
         send_query(d, 0).start()
     for copy in kv_copies:
+        copy.start()
+    for copy in local[:4]:
         copy.start()
     await_bytes(qbuf.at[0, pl.ds(1, steps - 1)], ql_sem.at[1])
     for first, count in [(1, 1)] + [(p, 2) for p in range(2, steps, 2)]:

time: 27.9 us -> 27.9 us (level)
  no operation moved by 1% of the time
where the time goes in v8:
time: 27.9 us; the launch traced here: 27.7 us
  Pallas kernels  26.9 us (96%)
  local copies, waits for them, and re-layouts  0.8 us (3%)
    pallas_call x1, Pallas kernels, on_device(): pl.pallas_call(functools.partial(kernel, n, pair), out_shape=pltpu.VMEM((...  26.9 us
    unnamed x1, local copies, waits for them, and re-layouts  0.8 us

profile of v8, /device:TPU:1, one launch (start us, length us, event | category | flops | bytes accessed | tf_op | source)
XLA Modules:
  0.0 27.7 jit_solution(2441925074758056093)
XLA Ops:
  0.0 26.9 %shard_map.73 = bf16[128,2048]{1,0:T(8,128)(2,1)S(1)} custom-call(bf16[128,2048]{1,0:T(8,128)(2,1)} %q_hbm.1, bf16[128,256]{1,0:T(8,128)(2,1)} %nk_hbm.1, bf16[128,256]{1,0:T(8,128)(2,1)} %nv_hbm.1, bf16[1024,256]{1,0:T(8,128)(2,1)} %ck_hbm.1, bf16[1024,256]{1,0:T(8,128)(2,1)} %cv_hbm.1, s32[4]{0:T(128)} %valid_hbm.1, s32[4]{0:T(128)} %block_hbm.1), custom_call_target="tpu_custom_call" | custom-call | tf_op jit(solution)/shard_map/pallas_call | solution.py:365
  26.9 0.8 %copy.9 = bf16[128,2048]{1,0:T(8,128)(2,1)} copy(bf16[128,2048]{1,0:T(8,128)(2,1)S(1)} %shard_map.73) | data formatting | bytes 1048576
